TPU v7x, 32 devices: a whole 2x2x4 slice. The times are simulated.
32 devices in a mesh: section: 2 (over core), group: 4 (over y, x), expert: 4 (over z).
Axes of the slice: x: 2, y: 2, z: 4, core: 2. Of those that a mesh axis runs over, the one named last changes fastest.
Arguments:
- tokens: bfloat16 [8, 256, 2048], P('group', 'expert'), parts along dimension 0
- chosen: int32 [2, 8, 1, 4], P('section', 'group'), parts along dimension 1, may hold values from 0 to 255, as said below
- norm_gain: float32 [2, 2048], P('section'), may hold values from 0.25 to 1.75
- router: bfloat16 [2, 2048, 1], P('section'), may hold values from -0.25 to 0.25
- w_in: bfloat16 [2, 4, 2048, 2048], P('section', 'expert'), may hold values from -0.125 to 0.125
- w_out: bfloat16 [2, 4, 2048, 2048], P('section', 'expert'), may hold values from -0.0625 to 0.0625
Outputs:
- outputs: bfloat16 [2, 8, 256, 2048], P('section', 'group', 'expert'), parts along dimension 1
There are 4 independent parts, one for each index of `group`. A program takes and returns all parts, laid end to end along the dimension named above; an argument that names none is the same for every part. Nothing has to cross between parts.
Inputs may be any that keep to these rules, and one draw needn't show every extreme that they name: `chosen`: for each section, micro-batch and expert the 4 indices are distinct and in no particular order. Of one device's tokens (an aligned block of 64 indices) an expert chooses at most 2; in every draw some expert chooses exactly 2 from some block.
All inputs are finite; a program needn't handle non-finite values.
Results may differ from a plain program's by a relative error of at most 0.001.
Values may be sent and summed in bfloat16 or wider, within the bound.
A program may use at most 64 MiB of HBM per device.

v0:
```python
import functools

import jax
import jax.numpy as jnp
from jax import lax
from jax.experimental import pallas as pl
from jax.experimental.pallas import tpu as pltpu
from jax.sharding import PartitionSpec as P

F32 = jnp.float32
BF16 = jnp.bfloat16
EPS = 1e-06
PARTS = 3


def row_iota(shape):
    return lax.broadcasted_iota(jnp.int32, shape, 0)


def lane_iota(shape):
    return lax.broadcasted_iota(jnp.int32, shape, 1)


def split_three(value):
    high = value.astype(BF16)
    rest = value - high.astype(F32)
    mid = rest.astype(BF16)
    low = (rest - mid.astype(F32)).astype(BF16)
    return jnp.concatenate([high, mid, low], axis=0)


def relay_kernel(
    dims,
    tok_hbm,
    chosen_hbm,
    gain_hbm,
    router_hbm,
    w1_hbm,
    w2_hbm,
    out_v,
    chosen_ref,
    gain_ref,
    router_ref,
    tok_v,
    w1_v,
    w2_v,
    rows_buf,
    x_v,
    acc_v,
    hid_v,
    part_send,
    part_recv,
    part_last,
    c_v,
    c_recv,
    ids_send,
    ids_recv,
    small_sem,
    tok_sem,
    w1_sem,
    w2_sem,
    rows_ssem,
    rows_rsem,
    part_ssem,
    part_rsem,
    last_ssem,
    last_rsem,
    misc_ssem,
    misc_rsem,
):
    micro, tok_rows, width, owners, cap, chunks, step = dims
    rows = micro * cap
    total = owners * tok_rows
    section = lax.axis_index("section")
    me = lax.axis_index("expert")

    def copy_to(src, dst, ssem, rsem, sec, exp):
        return pltpu.make_async_remote_copy(
            src_ref=src,
            dst_ref=dst,
            send_sem=ssem,
            recv_sem=rsem,
            device_id={"section": sec, "expert": exp},
            device_id_type=pl.DeviceIdType.MESH,
        )

    barrier = pltpu.get_barrier_semaphore()
    for o in range(1, owners):
        pl.semaphore_signal(
            barrier,
            inc=1,
            device_id={"section": section, "expert": lax.rem(me + o, owners)},
            device_id_type=pl.DeviceIdType.MESH,
        )
    for o in range(owners):
        pl.semaphore_signal(
            barrier,
            inc=1,
            device_id={"section": 1 - section, "expert": lax.rem(me + o, owners)},
            device_id_type=pl.DeviceIdType.MESH,
        )
    tok_copies = [
        pltpu.make_async_copy(
            tok_hbm.at[m], tok_v.at[pl.ds(m * tok_rows, tok_rows)], tok_sem.at[m]
        )
        for m in range(micro)
    ]
    small_copies = [
        pltpu.make_async_copy(chosen_hbm, chosen_ref, small_sem.at[0]),
        pltpu.make_async_copy(gain_hbm, gain_ref, small_sem.at[1]),
        pltpu.make_async_copy(router_hbm, router_ref, small_sem.at[2]),
    ]
    for c in small_copies[:1] + tok_copies + small_copies[1:]:
        c.start()
    w1_copies = [
        pltpu.make_async_copy(
            w1_hbm.at[0, 0, pl.ds(k * step, step)], w1_v.at[pl.ds(k * step, step)], w1_sem.at[k]
        )
        for k in range(chunks)
    ]
    w2_copies = [
        pltpu.make_async_copy(
            w2_hbm.at[0, 0, :, pl.ds(k * step, step)], w2_v.at[k], w2_sem.at[k]
        )
        for k in range(chunks)
    ]

    small_copies[0].wait()
    id_col = jnp.full((rows, 128), -1, jnp.int32)
    id_row = jnp.full((rows, 128), -1, jnp.int32)
    for r in range(rows):
        ident = chosen_ref[0, r // cap, 0, r % cap] + (r // cap) * total
        id_col = jnp.where(row_iota((rows, 128)) == r, ident, id_col)
        lanes = lane_iota((rows, 128))
        for part in range(PARTS):
            id_row = jnp.where(lanes == part * rows + r, ident, id_row)
    ids_send[...] = id_row

    def own_ids(iota):
        value = iota + me * tok_rows
        for m in range(1, micro):
            value = value + jnp.where(iota >= m * tok_rows, total - tok_rows, 0)
        return value

    for c in tok_copies:
        c.wait()
    for c in w1_copies + w2_copies:
        c.start()
    mine = own_ids(lane_iota((rows, micro * tok_rows)))
    onehot = (mine == id_col[:, :1]).astype(F32).astype(BF16)
    rows_buf[me] = jnp.dot(onehot, tok_v[...], preferred_element_type=F32).astype(BF16)
    pl.semaphore_wait(barrier, 2 * owners - 1)

    row_copies = [
        copy_to(
            rows_buf.at[me], rows_buf.at[me], rows_ssem.at[o], rows_rsem.at[me],
            section, lax.rem(me + o, owners),
        )
        for o in range(1, owners)
    ]

    def gathered_rows():
        for o in range(1, owners):
            p = lax.rem(me + o, owners)
            copy_to(
                rows_buf.at[p], rows_buf.at[p], rows_ssem.at[o], rows_rsem.at[p], section, p
            ).wait_recv()
        value = rows_buf[0].astype(F32)
        for p in range(1, owners):
            value = value + rows_buf[p].astype(F32)
        return value

    def placed(base, ids_row, contrib):
        mine = own_ids(row_iota((micro * tok_rows, PARTS * rows)))
        hit = (mine == ids_row[:1, : PARTS * rows]).astype(F32).astype(BF16)
        added = jnp.dot(hit, split_three(contrib), preferred_element_type=F32)
        return (base.astype(F32) + added).astype(BF16)

    def second_matmul(j, gate):
        w2_copies[j].wait()
        return (
            jnp.dot(hid_v[...], w2_v[j], preferred_element_type=F32) * gate
        ).astype(BF16)

    @pl.when(section == 0)
    def _():
        for c in row_copies:
            c.start()
        for c in row_copies:
            c.wait_send()
        ids_copy = copy_to(ids_send, ids_recv, misc_ssem.at[0], misc_rsem.at[0], 1, me)
        ids_copy.start()
        for c in small_copies[1:]:
            c.wait()
        floats = gathered_rows()
        inverse = lax.rsqrt(jnp.mean(floats * floats, axis=-1, keepdims=True) + EPS)
        normed = (floats * inverse * gain_ref[...]).astype(BF16)
        x_v[...] = normed
        score = jnp.sum(normed.astype(F32) * router_ref[...].astype(F32), axis=-1, keepdims=True)
        gate = jax.nn.sigmoid(score)
        for k in range(chunks):
            w1_copies[k].wait()
            piece = jnp.dot(
                x_v[:, k * step : (k + 1) * step],
                w1_v[k * step : (k + 1) * step, :],
                preferred_element_type=F32,
            )
            acc_v[...] = piece if k == 0 else acc_v[...] + piece
        hid_v[...] = jax.nn.gelu(acc_v[...], approximate=True).astype(BF16)
        sent = []
        for j in range(chunks):
            part_send[j] = second_matmul(j, gate)
            for o in list(range(1, owners)) + [0]:
                c = copy_to(
                    part_send.at[j], part_recv.at[me, j], part_ssem.at[o, j],
                    part_rsem.at[me, j], 1, lax.rem(me + o, owners),
                )
                c.start()
                sent.append(c)
        back = copy_to(c_v, c_recv, misc_ssem.at[1], misc_rsem.at[1], 0, me)
        back.wait_recv()
        out_v[...] = placed(tok_v[...], id_row, c_recv[...])
        for c in sent:
            c.wait_send()
        ids_copy.wait_send()

    @pl.when(section != 0)
    def _():
        copy_to(ids_send, ids_recv, misc_ssem.at[0], misc_rsem.at[0], 1, me).wait_recv()
        for c in row_copies:
            c.start()
        for c in row_copies:
            c.wait_send()
        for c in small_copies[1:]:
            c.wait()
        raw = gathered_rows()
        before = ids_recv[...]
        match = ((id_col == before) & (lane_iota((rows, 128)) < rows)).astype(F32)
        for c in w1_copies:
            c.wait()
        squares = jnp.zeros((rows, 128), F32)
        scores = jnp.zeros((rows, 128), F32)
        for k in range(chunks):
            for p in range(owners):
                copy_to(
                    part_send.at[k], part_recv.at[p, k], part_ssem.at[0, k],
                    part_rsem.at[p, k], 1, p,
                ).wait_recv()
            span = slice(k * step, (k + 1) * step)
            contrib = part_recv[0, k].astype(F32)
            for p in range(1, owners):
                contrib = contrib + part_recv[p, k].astype(F32)
            c_v[:, span] = contrib
            act = raw[:, span]
            added = match[:, 0:1] * contrib[0:1, :]
            for r in range(1, rows):
                added = added + match[:, r : r + 1] * contrib[r : r + 1, :]
            act = (act + added).astype(BF16).astype(F32)
            scaled = (act * gain_ref[:, span]).astype(BF16)
            weighted = scaled.astype(F32) * router_ref[:, span].astype(F32)
            square = act * act
            for b in range(step // 128):
                squares = squares + square[:, b * 128 : (b + 1) * 128]
                scores = scores + weighted[:, b * 128 : (b + 1) * 128]
            piece = jnp.dot(scaled, w1_v[span, :], preferred_element_type=F32)
            acc_v[...] = piece if k == 0 else acc_v[...] + piece
        back = copy_to(c_v, c_recv, misc_ssem.at[1], misc_rsem.at[1], 0, me)
        back.start()
        inverse = lax.rsqrt(jnp.sum(squares, axis=-1, keepdims=True) / width + EPS)
        gate = jax.nn.sigmoid(jnp.sum(scores, axis=-1, keepdims=True) * inverse)
        hid_v[...] = jax.nn.gelu(acc_v[...] * inverse, approximate=True).astype(BF16)
        sent = []
        for j in range(chunks):
            part_send[j] = second_matmul(j, gate)
            for o in range(1, owners):
                c = copy_to(
                    part_send.at[j], part_last.at[me, j], last_ssem.at[o, j],
                    last_rsem.at[me, j], 1, lax.rem(me + o, owners),
                )
                c.start()
                sent.append(c)
            part_last[me, j] = part_send[j]
        out_v[...] = placed(tok_v[...], before, c_v[...])
        for j in range(chunks):
            span = slice(j * step, (j + 1) * step)
            for o in range(1, owners):
                p = lax.rem(me + o, owners)
                copy_to(
                    part_send.at[j], part_last.at[p, j], last_ssem.at[o, j],
                    last_rsem.at[p, j], 1, p,
                ).wait_recv()
            contrib = part_last[0, j].astype(F32)
            for p in range(1, owners):
                contrib = contrib + part_last[p, j].astype(F32)
            out_v[:, span] = placed(out_v[:, span], id_row, contrib)
        for c in sent:
            c.wait_send()
        back.wait_send()


def fused(tokens, chosen, norm_gain, router, w_in, w_out):
    micro, tok_rows, width = tokens.shape
    owners = lax.axis_size("expert")
    cap = chosen.shape[3]
    hidden = w_in.shape[3]
    rows = micro * cap
    chunks = 4
    step = width // chunks
    dims = (micro, tok_rows, width, owners, cap, chunks, step)
    vmem = pl.BlockSpec(memory_space=pltpu.VMEM)
    hbm = pl.BlockSpec(memory_space=pltpu.HBM)
    dma = pltpu.SemaphoreType.DMA
    result = pl.pallas_call(
        functools.partial(relay_kernel, dims),
        out_shape=pltpu.VMEM((micro * tok_rows, width), BF16),
        in_specs=[hbm] * 6,
        out_specs=vmem,
        scratch_shapes=[
            pltpu.SMEM((1, micro, 1, cap), jnp.int32),
            pltpu.VMEM((1, width), F32),
            pltpu.VMEM((1, width), BF16),
            pltpu.VMEM((micro * tok_rows, width), BF16),
            pltpu.VMEM((width, hidden), BF16),
            pltpu.VMEM((chunks, hidden, step), BF16),
            pltpu.VMEM((owners, rows, width), BF16),
            pltpu.VMEM((rows, width), BF16),
            pltpu.VMEM((rows, hidden), F32),
            pltpu.VMEM((rows, hidden), BF16),
            pltpu.VMEM((chunks, rows, step), BF16),
            pltpu.VMEM((owners, chunks, rows, step), BF16),
            pltpu.VMEM((owners, chunks, rows, step), BF16),
            pltpu.VMEM((rows, width), F32),
            pltpu.VMEM((rows, width), F32),
            pltpu.VMEM((rows, 128), jnp.int32),
            pltpu.VMEM((rows, 128), jnp.int32),
            dma((3,)),
            dma((micro,)),
            dma((chunks,)),
            dma((chunks,)),
            dma((owners,)),
            dma((owners,)),
            dma((owners, chunks)),
            dma((owners, chunks)),
            dma((owners, chunks)),
            dma((owners, chunks)),
            dma((2,)),
            dma((2,)),
        ],
        compiler_params=pltpu.CompilerParams(
            collective_id=0, has_side_effects=True, vmem_limit_bytes=60 * 1024 * 1024
        ),
    )(tokens, chosen, norm_gain, router[:, :, 0], w_in, w_out)
    return result.reshape(1, micro, tok_rows, width)


def passed_along(value, axis, steps):
    count = lax.axis_size(axis)
    leading, last = (max(0, -steps), min(count, count - steps))
    return lax.ppermute(value, axis, [(source, source + steps) for source in range(leading, last)])


def moe_layer(
    current, picks_now, gain_row, router_cols, w_first, w_second, device, owners, shards_each
):
    tok_rows, width = current.shape
    experts, capacity = picks_now.shape
    slots = 2 * capacity // owners
    floats = current.astype(jnp.float32)
    inverse_rms = lax.rsqrt(jnp.mean(floats * floats, axis=-1, keepdims=True) + 1e-06)
    normed = (floats * inverse_rms * gain_row).astype(jnp.bfloat16)
    gate_all = jax.nn.sigmoid(jnp.dot(normed, router_cols, preferred_element_type=jnp.float32))
    owner_of = picks_now // tok_rows
    onehot = (owner_of[:, :, None] == jnp.arange(owners, dtype=jnp.int32)[None, None, :]).astype(
        jnp.int32
    )
    order_slot = jnp.cumsum(onehot, axis=1) - 1
    slot_of = jnp.sum(order_slot * onehot, axis=2)
    is_mine = owner_of == device
    local_idx = picks_now - device * tok_rows
    slot_hit = (
        (slot_of[:, :, None] == jnp.arange(slots, dtype=jnp.int32)[None, None, :])
        & is_mine[:, :, None]
    ).astype(jnp.float32)
    tok_hit = (
        local_idx[:, :, None] == jnp.arange(tok_rows, dtype=jnp.int32)[None, None, :]
    ).astype(jnp.float32)
    selector = jnp.einsum("xcs,xct->xst", slot_hit, tok_hit)
    flat_select = selector.reshape(experts * slots, tok_rows)
    gate_slot = jnp.einsum("xst,tx->xs", selector, gate_all, precision=lax.Precision.HIGHEST)
    dispatched = jnp.dot(
        flat_select.astype(jnp.bfloat16), normed, preferred_element_type=jnp.float32
    ).astype(jnp.bfloat16)
    outgoing = jnp.broadcast_to(
        dispatched.reshape(experts, 1, slots, width), (experts, shards_each, slots, width)
    ).reshape(owners, slots, width)
    arrived = lax.all_to_all(outgoing, "expert", split_axis=0, concat_axis=0, tiled=True)
    item_count = arrived.shape[1]
    flat_rows = arrived.reshape(-1, width)
    hidden = jax.nn.gelu(
        jnp.dot(flat_rows, w_first, preferred_element_type=jnp.float32), approximate=True
    ).astype(jnp.bfloat16)
    partial_value = jnp.dot(hidden, w_second, preferred_element_type=jnp.float32).reshape(
        owners, item_count, width
    )
    returned = lax.all_to_all(partial_value, "expert", split_axis=0, concat_axis=0, tiled=True)
    summed = returned.reshape(experts, shards_each, slots, width).sum(axis=1)
    weighted = summed * gate_slot[:, :, None]
    contrib = jnp.dot(
        flat_select.T, weighted.reshape(experts * slots, width), precision=lax.Precision.HIGHEST
    )
    return (floats + contrib).astype(jnp.bfloat16)


def fits(tokens, chosen, w_in, sections, owners):
    micro, tok_rows, width = tokens.shape
    experts, cap = chosen.shape[2:]
    rows = micro * cap
    whole_tiles = rows % 8 == 0 and width % 512 == 0 and w_in.shape[3] % 256 == 0
    return sections == 2 and experts == 1 and whole_tiles and rows * PARTS <= 128 and owners <= 8


def local(tokens, chosen, norm_gain, router, w_in, w_out):
    sections = lax.axis_size("section")
    owners = lax.axis_size("expert")
    if fits(tokens, chosen, w_in, sections, owners):
        return fused(tokens, chosen, norm_gain, router, w_in, w_out)
    section_index = lax.axis_index("section")
    device = lax.axis_index("expert")
    micro_count, tok_rows, width = tokens.shape
    experts = chosen.shape[2]
    shards_each = owners // experts
    gain_row = norm_gain[0]
    router_cols = router[0]
    w_first = w_in[0, 0]
    w_second = w_out[0, 0]
    outputs = jnp.zeros((1, micro_count, tok_rows, width), jnp.bfloat16)
    received = jnp.zeros((tok_rows, width), jnp.bfloat16)
    tick_count = micro_count + sections - 1
    for tick_index in range(tick_count):
        batch_index = tick_index - section_index
        clipped = jnp.clip(batch_index, 0, micro_count - 1)
        fresh_input = tokens[min(tick_index, micro_count - 1)]
        current = jnp.where(section_index == 0, fresh_input, received)
        picks_now = lax.dynamic_index_in_dim(chosen[0], clipped, 0, keepdims=False)
        layer_out = moe_layer(
            current,
            picks_now,
            gain_row,
            router_cols,
            w_first,
            w_second,
            device,
            owners,
            shards_each,
        )
        in_range = (batch_index >= 0) & (batch_index < micro_count)
        previous = lax.dynamic_index_in_dim(outputs[0], clipped, 0, keepdims=False)
        written = jnp.where(in_range, layer_out, previous)
        outputs = lax.dynamic_update_index_in_dim(outputs, written[None, None], clipped, 1)
        if tick_index + 1 < tick_count:
            received = passed_along(layer_out, "section", 1)
    return outputs


def solution(mesh):
    placed = (
        P("group", "expert", None),
        P("section", "group", None, None),
        P("section", None),
        P("section", None, None),
        P("section", "expert", None, None),
        P("section", "expert", None, None),
    )
    return jax.shard_map(
        local,
        mesh=mesh,
        in_specs=placed,
        out_specs=P("section", "group", "expert", None),
        check_vma=False,
    )
```

profile of v0, /device:TPU:1, one launch (start us, length us, event | category | flops | bytes accessed | tf_op | source)
XLA Modules:
  0.0 20.9 jit_solution(7883598041145291188)
XLA Ops:
  0.0 20.1 %shard_map.64 = bf16[128,2048]{1,0:T(8,128)(2,1)S(1)} custom-call(bf16[2,64,2048]{2,1,0:T(8,128)(2,1)} %tok_hbm.1, s32[1,2,1,4]{3,2,1,0:T(1,128)} %chosen_hbm.1, f32[1,2048]{1,0:T(1,128)} %gain_hbm.1, bf16[1,2048]{1,0:T(2,128)(2,1)} %bitcast.3, bf16[1,1,2048,2048]{3,2,1,0:T(8,128)(2,1)} %w1_hbm.1, bf16[1,1,2048,2048]{3,2,1,0:T(8,128)(2,1)} %w2_hbm.1), custom_call_target="tpu_custom_call" | custom-call | tf_op jit(solution)/shard_map/pallas_call | solution.py:313
  20.1 0.8 %copy.8 = bf16[1,2,64,2048]{3,2,1,0:T(8,128)(2,1)} copy(bf16[1,2,64,2048]{3,2,1,0:T(8,128)(2,1)S(1)} %bitcast.2) | data formatting | bytes 1048576
where the time goes:
time: 21 us; the launch traced here: 20.9 us
  Pallas kernels  20.1 us (96%)
  local copies, waits for them, and re-layouts  0.8 us (4%)
    pallas_call x1, Pallas kernels, fused(): pl.pallas_call(functools.partial(relay_kernel, dims), out_shape=pltpu.VME...  20.1 us
    unnamed x1, local copies, waits for them, and re-layouts  0.8 us

commit v1 on v0

--- a/solution.py
+++ b/solution.py
@@ -55,18 +55,16 @@
     c_recv,
     ids_send,
     ids_recv,
+    rows_rsem,
+    part_rsem,
+    misc_rsem,
     small_sem,
     tok_sem,
     w1_sem,
     w2_sem,
     rows_ssem,
-    rows_rsem,
     part_ssem,
-    part_rsem,
-    last_ssem,
-    last_rsem,
     misc_ssem,
-    misc_rsem,
 ):
     micro, tok_rows, width, owners, cap, chunks, step = dims
     rows = micro * cap
@@ -83,6 +81,15 @@
             device_id={"section": sec, "expert": exp},
             device_id_type=pl.DeviceIdType.MESH,
         )
+
+    def all_of(ref, sem):
+        return pltpu.make_async_copy(ref, ref, sem)
+
+    def peer(k):
+        low = k + jnp.where(k >= me, 1, 0)
+        top = owners - 1 - k
+        high = top - jnp.where(top <= me, 1, 0)
+        return jnp.where(2 * me < owners, high, low)
 
     barrier = pltpu.get_barrier_semaphore()
     for o in range(1, owners):
@@ -153,18 +160,13 @@
 
     row_copies = [
         copy_to(
-            rows_buf.at[me], rows_buf.at[me], rows_ssem.at[o], rows_rsem.at[me],
-            section, lax.rem(me + o, owners),
-        )
-        for o in range(1, owners)
+            rows_buf.at[me], rows_buf.at[me], rows_ssem, rows_rsem, section, peer(k)
+        )
+        for k in range(owners - 1)
     ]
 
     def gathered_rows():
-        for o in range(1, owners):
-            p = lax.rem(me + o, owners)
-            copy_to(
-                rows_buf.at[p], rows_buf.at[p], rows_ssem.at[o], rows_rsem.at[p], section, p
-            ).wait_recv()
+        all_of(rows_buf.at[pl.ds(0, owners - 1)], rows_rsem).wait()
         value = rows_buf[0].astype(F32)
         for p in range(1, owners):
             value = value + rows_buf[p].astype(F32)
@@ -186,8 +188,7 @@
     def _():
         for c in row_copies:
             c.start()
-        for c in row_copies:
-            c.wait_send()
+        all_of(rows_buf.at[pl.ds(0, owners - 1)], rows_ssem).wait()
         ids_copy = copy_to(ids_send, ids_recv, misc_ssem.at[0], misc_rsem.at[0], 1, me)
         ids_copy.start()
         for c in small_copies[1:]:
@@ -207,21 +208,16 @@
             )
             acc_v[...] = piece if k == 0 else acc_v[...] + piece
         hid_v[...] = jax.nn.gelu(acc_v[...], approximate=True).astype(BF16)
-        sent = []
         for j in range(chunks):
             part_send[j] = second_matmul(j, gate)
-            for o in list(range(1, owners)) + [0]:
-                c = copy_to(
-                    part_send.at[j], part_recv.at[me, j], part_ssem.at[o, j],
-                    part_rsem.at[me, j], 1, lax.rem(me + o, owners),
-                )
-                c.start()
-                sent.append(c)
+            for p in [peer(k) for k in range(owners - 1)] + [me]:
+                copy_to(
+                    part_send.at[j], part_recv.at[j, me], part_ssem, part_rsem.at[j], 1, p
+                ).start()
         back = copy_to(c_v, c_recv, misc_ssem.at[1], misc_rsem.at[1], 0, me)
         back.wait_recv()
         out_v[...] = placed(tok_v[...], id_row, c_recv[...])
-        for c in sent:
-            c.wait_send()
+        all_of(part_recv, part_ssem).wait()
         ids_copy.wait_send()
 
     @pl.when(section != 0)
@@ -229,8 +225,7 @@
         copy_to(ids_send, ids_recv, misc_ssem.at[0], misc_rsem.at[0], 1, me).wait_recv()
         for c in row_copies:
             c.start()
-        for c in row_copies:
-            c.wait_send()
+        all_of(rows_buf.at[pl.ds(0, owners - 1)], rows_ssem).wait()
         for c in small_copies[1:]:
             c.wait()
         raw = gathered_rows()
@@ -241,15 +236,11 @@
         squares = jnp.zeros((rows, 128), F32)
         scores = jnp.zeros((rows, 128), F32)
         for k in range(chunks):
-            for p in range(owners):
-                copy_to(
-                    part_send.at[k], part_recv.at[p, k], part_ssem.at[0, k],
-                    part_rsem.at[p, k], 1, p,
-                ).wait_recv()
+            all_of(part_recv.at[k], part_rsem.at[k]).wait()
             span = slice(k * step, (k + 1) * step)
-            contrib = part_recv[0, k].astype(F32)
+            contrib = part_recv[k, 0].astype(F32)
             for p in range(1, owners):
-                contrib = contrib + part_recv[p, k].astype(F32)
+                contrib = contrib + part_recv[k, p].astype(F32)
             c_v[:, span] = contrib
             act = raw[:, span]
             added = match[:, 0:1] * contrib[0:1, :]
@@ -269,33 +260,40 @@
         inverse = lax.rsqrt(jnp.sum(squares, axis=-1, keepdims=True) / width + EPS)
         gate = jax.nn.sigmoid(jnp.sum(scores, axis=-1, keepdims=True) * inverse)
         hid_v[...] = jax.nn.gelu(acc_v[...] * inverse, approximate=True).astype(BF16)
-        sent = []
         for j in range(chunks):
             part_send[j] = second_matmul(j, gate)
-            for o in range(1, owners):
-                c = copy_to(
-                    part_send.at[j], part_last.at[me, j], last_ssem.at[o, j],
-                    last_rsem.at[me, j], 1, lax.rem(me + o, owners),
-                )
-                c.start()
-                sent.append(c)
-            part_last[me, j] = part_send[j]
+            for k in range(owners - 1):
+                copy_to(
+                    part_send.at[j], part_last.at[j, me], part_ssem, part_rsem.at[chunks + j],
+                    1, peer(k),
+                ).start()
+            part_last[j, me] = part_send[j]
         out_v[...] = placed(tok_v[...], before, c_v[...])
         for j in range(chunks):
             span = slice(j * step, (j + 1) * step)
-            for o in range(1, owners):
-                p = lax.rem(me + o, owners)
-                copy_to(
-                    part_send.at[j], part_last.at[p, j], last_ssem.at[o, j],
-                    last_rsem.at[p, j], 1, p,
-                ).wait_recv()
-            contrib = part_last[0, j].astype(F32)
+            all_of(part_last.at[j, pl.ds(0, owners - 1)], part_rsem.at[chunks + j]).wait()
+            contrib = part_last[j, 0].astype(F32)
             for p in range(1, owners):
-                contrib = contrib + part_last[p, j].astype(F32)
+                contrib = contrib + part_last[j, p].astype(F32)
             out_v[:, span] = placed(out_v[:, span], id_row, contrib)
-        for c in sent:
-            c.wait_send()
+        all_of(part_last.at[:, pl.ds(0, owners - 1)], part_ssem).wait()
         back.wait_send()
+
+
+def scoped_kernel(dims, *refs):
+    micro, chunks = dims[0], dims[5]
+    dma = pltpu.SemaphoreType.DMA
+
+    pl.run_scoped(
+        lambda *sems: relay_kernel(dims, *refs, *sems),
+        dma((3,)),
+        dma((micro,)),
+        dma((chunks,)),
+        dma((chunks,)),
+        dma,
+        dma,
+        dma((2,)),
+    )
 
 
 def fused(tokens, chosen, norm_gain, router, w_in, w_out):
@@ -311,7 +309,7 @@
     hbm = pl.BlockSpec(memory_space=pltpu.HBM)
     dma = pltpu.SemaphoreType.DMA
     result = pl.pallas_call(
-        functools.partial(relay_kernel, dims),
+        functools.partial(scoped_kernel, dims),
         out_shape=pltpu.VMEM((micro * tok_rows, width), BF16),
         in_specs=[hbm] * 6,
         out_specs=vmem,
@@ -327,23 +325,14 @@
             pltpu.VMEM((rows, hidden), F32),
             pltpu.VMEM((rows, hidden), BF16),
             pltpu.VMEM((chunks, rows, step), BF16),
-            pltpu.VMEM((owners, chunks, rows, step), BF16),
-            pltpu.VMEM((owners, chunks, rows, step), BF16),
+            pltpu.VMEM((chunks, owners, rows, step), BF16),
+            pltpu.VMEM((chunks, owners, rows, step), BF16),
             pltpu.VMEM((rows, width), F32),
             pltpu.VMEM((rows, width), F32),
             pltpu.VMEM((rows, 128), jnp.int32),
             pltpu.VMEM((rows, 128), jnp.int32),
-            dma((3,)),
-            dma((micro,)),
-            dma((chunks,)),
-            dma((chunks,)),
-            dma((owners,)),
-            dma((owners,)),
-            dma((owners, chunks)),
-            dma((owners, chunks)),
-            dma((owners, chunks)),
-            dma((owners, chunks)),
-            dma((2,)),
+            dma,
+            dma((2 * chunks,)),
             dma((2,)),
         ],
         compiler_params=pltpu.CompilerParams(

time: 21 us -> 20.1 us (0.957)
  Pallas kernels: 20.1 us -> 19.2 us
    pallas_call x1, Pallas kernels: 20.1 us -> 19.2 us  [fused(): pl.pallas_call(functools.partial(scoped_kernel, dims), out_shape=pltpu.VM...]
where the time goes in v1:
time: 20.1 us; the launch traced here: 20 us
  Pallas kernels  19.2 us (96%)
  local copies, waits for them, and re-layouts  0.8 us (4%)
    pallas_call x1, Pallas kernels, fused(): pl.pallas_call(functools.partial(scoped_kernel, dims), out_shape=pltpu.VM...  19.2 us
    unnamed x1, local copies, waits for them, and re-layouts  0.8 us

profile of v1, /device:TPU:1, one launch (start us, length us, event | category | flops | bytes accessed | tf_op | source)
XLA Modules:
  0.0 20.0 jit_solution(10177478632244152950)
XLA Ops:
  0.0 19.2 %shard_map.64 = bf16[128,2048]{1,0:T(8,128)(2,1)S(1)} custom-call(bf16[2,64,2048]{2,1,0:T(8,128)(2,1)} %refs_0_.1, s32[1,2,1,4]{3,2,1,0:T(1,128)} %refs_1_.1, f32[1,2048]{1,0:T(1,128)} %refs_2_.1, bf16[1,2048]{1,0:T(2,128)(2,1)} %bitcast.3, bf16[1,1,2048,2048]{3,2,1,0:T(8,128)(2,1)} %refs_4_.1, bf16[1,1,2048,2048]{3,2,1,0:T(8,128)(2,1)} %refs_5_.1), custom_call_target="tpu_custom_call" | custom-call | tf_op jit(solution)/shard_map/pallas_call | solution.py:311
  19.2 0.8 %copy.8 = bf16[1,2,64,2048]{3,2,1,0:T(8,128)(2,1)} copy(bf16[1,2,64,2048]{3,2,1,0:T(8,128)(2,1)S(1)} %bitcast.2) | data formatting | bytes 1048576

commit v2 on v1

v2 whole, which is shorter than its diff:
```python
import functools

import jax
import jax.numpy as jnp
from jax import lax
from jax.experimental import pallas as pl
from jax.experimental.pallas import tpu as pltpu
from jax.sharding import PartitionSpec as P

F32 = jnp.float32
BF16 = jnp.bfloat16
EPS = 1e-06
TILE = 256
SEND_TILES = (1, 1, 2, 2, 1, 1)
LAST_TILES = (2, 2, 2, 1, 1)


def row_iota(shape):
    return lax.broadcasted_iota(jnp.int32, shape, 0)


def lane_iota(shape):
    return lax.broadcasted_iota(jnp.int32, shape, 1)


def tile_at(index, count=1):
    return slice(index * TILE, (index + count) * TILE)


def pieces(sizes, tiles):
    found, start = [], 0
    for size in sizes:
        size = min(size, tiles - start)
        if size > 0:
            found.append((start, size))
            start += size
    while start < tiles:
        found.append((start, 1))
        start += 1
    return found


def relay_kernel(
    dims,
    tok_hbm,
    chosen_hbm,
    gain_hbm,
    router_hbm,
    w1_hbm,
    w2_hbm,
    out_v,
    chosen_ref,
    gain_ref,
    router_ref,
    tok_v,
    w1_v,
    w2_v,
    rows_buf,
    xf_v,
    part_send,
    part_recv,
    last_send,
    last_recv,
    c_v,
    c_recv,
    fin_v,
    ids_send,
    ids_recv,
    own_ref,
    rows_rsem,
    part_rsem,
    last_rsem,
    misc_rsem,
    sums,
    outs,
    small_sem,
    tok_sem,
    w1_sem,
    w2_sem,
    rows_ssem,
    part_ssem,
    misc_ssem,
):
    micro, tok_rows, width, hidden, owners, cap, slots = dims
    rows = micro * cap
    each = micro * slots
    items = owners * each
    total = owners * tok_rows
    tokens = micro * tok_rows
    in_tiles, hid_tiles = width // TILE, hidden // TILE
    send_pieces = pieces(SEND_TILES, in_tiles)
    last_pieces = pieces(LAST_TILES, in_tiles)
    section = lax.axis_index("section")
    me = lax.axis_index("expert")

    def copy_to(src, dst, ssem, rsem, sec, exp):
        return pltpu.make_async_remote_copy(
            src_ref=src,
            dst_ref=dst,
            send_sem=ssem,
            recv_sem=rsem,
            device_id={"section": sec, "expert": exp},
            device_id_type=pl.DeviceIdType.MESH,
        )

    def all_of(ref, sem):
        return pltpu.make_async_copy(ref, ref, sem)

    def peer(k):
        low = k + jnp.where(k >= me, 1, 0)
        top = owners - 1 - k
        high = top - jnp.where(top <= me, 1, 0)
        return jnp.where(2 * me < owners, high, low)

    staged = [0, 0]

    def multiply(acc, lhs, rhs, unit):
        register = staged[unit]
        staged[unit] = 1 - register
        pltpu.matmul_push_rhs(rhs, staging_register=register, mxu_index=unit)
        pltpu.matmul_acc_lhs(acc, lhs, load_staged_rhs=register)

    barrier = pltpu.get_barrier_semaphore()
    for o in range(1, owners):
        pl.semaphore_signal(
            barrier,
            inc=1,
            device_id={"section": section, "expert": lax.rem(me + o, owners)},
            device_id_type=pl.DeviceIdType.MESH,
        )
    for o in range(owners):
        pl.semaphore_signal(
            barrier,
            inc=1,
            device_id={"section": 1 - section, "expert": lax.rem(me + o, owners)},
            device_id_type=pl.DeviceIdType.MESH,
        )
    tok_copies = [
        pltpu.make_async_copy(
            tok_hbm.at[m], tok_v.at[pl.ds(m * tok_rows, tok_rows)], tok_sem.at[m]
        )
        for m in range(micro)
    ]
    small_copies = [
        pltpu.make_async_copy(chosen_hbm, chosen_ref, small_sem.at[0]),
        pltpu.make_async_copy(gain_hbm, gain_ref, small_sem.at[1]),
        pltpu.make_async_copy(router_hbm, router_ref, small_sem.at[2]),
    ]
    for c in small_copies[:1] + tok_copies + small_copies[1:]:
        c.start()
    parts = 4
    deep, half = width // parts, width // 2
    w1_copies = [
        pltpu.make_async_copy(
            w1_hbm.at[0, 0, pl.ds(k * deep, deep)], w1_v.at[pl.ds(k * deep, deep)], w1_sem
        )
        for k in range(parts)
    ]
    w2_copies = [
        pltpu.make_async_copy(
            w2_hbm.at[0, 0, :, pl.ds(k * half, half)],
            w2_v.at[:, pl.ds(k * half, half)],
            w2_sem.at[k],
        )
        for k in range(2)
    ]
    if tokens < TILE:
        tok_v[tokens:, :] = jnp.zeros((TILE - tokens, width), BF16)

    small_copies[0].wait()
    id_col = jnp.full((rows, 128), -1, jnp.int32)
    code_col = jnp.full((rows, 128), -1, jnp.int32)
    item_id = jnp.full((items, 128), -1, jnp.int32)
    own_id = jnp.full((items, 128), -1, jnp.int32)
    for m in range(micro):
        owner_of = []
        for c in range(cap):
            r = m * cap + c
            pick = chosen_ref[0, m, 0, c]
            ident = pick + m * total
            owner = lax.div(pick, jnp.int32(tok_rows))
            slot = jnp.int32(0)
            for earlier in owner_of:
                slot = slot + jnp.where(earlier == owner, 1, 0)
            owner_of.append(owner)
            inner = m * slots + slot
            id_col = jnp.where(row_iota((rows, 128)) == r, ident, id_col)
            code_col = jnp.where(row_iota((rows, 128)) == r, owner * slots + slot, code_col)
            item_id = jnp.where(row_iota((items, 128)) == owner * each + inner, ident, item_id)
            at = jnp.where(owner == me, inner, -1)
            own_id = jnp.where(row_iota((items, 128)) == at, ident, own_id)
    ids_send[...] = id_col
    own_ref[...] = own_id

    lanes = lane_iota((items, TILE))
    lane_id = lanes + me * tok_rows
    for m in range(1, micro):
        lane_id = lane_id + jnp.where(lanes >= m * tok_rows, total - tok_rows, 0)
    lane_id = jnp.where(lanes < tokens, lane_id, -2)
    pick_lhs = (
        (lane_id == jnp.concatenate([own_id] * (TILE // 128), axis=1)).astype(F32).astype(BF16)
    )

    for c in tok_copies:
        c.wait()
    for c in w1_copies + w2_copies:
        c.start()

    def pick_rows(first, count):
        for n in range(first, first + count):
            multiply(sums[n], pick_lhs, tok_v[:, tile_at(n)], n % 2)
        for n in range(first, first + count):
            rows_buf[me, :, tile_at(n)] = pltpu.matmul_pop(sums[n])[:each].astype(BF16)

    def row_sends(first, count):
        span = tile_at(first, count)
        return [
            copy_to(
                rows_buf.at[me, :, span], rows_buf.at[me, :, span], rows_ssem, rows_rsem,
                section, peer(k),
            )
            for k in range(owners - 1)
        ]

    def gathered_rows():
        all_of(rows_buf.at[pl.ds(0, owners - 1)], rows_rsem).wait()
        for p in range(owners):
            xf_v[p * each : (p + 1) * each, :] = rows_buf[p].astype(F32)

    def folded(value, start):
        for b in range(TILE // 128):
            start = start + value[:, b * 128 : (b + 1) * 128]
        return start

    def scaled_tile(act, tile, stats):
        span = tile_at(tile)
        scaled = (act * gain_ref[:, span]).astype(BF16)
        weighted = scaled.astype(F32) * router_ref[:, span].astype(F32)
        return scaled, (folded(act * act, stats[0]), folded(weighted, stats[1]))

    def closing(stats):
        inverse = lax.rsqrt(jnp.sum(stats[0], axis=-1, keepdims=True) / width + EPS)
        score = jnp.sum(stats[1], axis=-1, keepdims=True)
        gate = jax.nn.sigmoid(jnp.where(inverse > 0, score * inverse, 0.0))
        return inverse, gate

    hid = {}

    def finish(pair, inverse):
        for n in (2 * pair, 2 * pair + 1):
            value = jnp.where(inverse > 0, pltpu.matmul_pop(sums[n]) * inverse, 0.0)
            hid[n] = jax.nn.gelu(value, approximate=True).astype(BF16)

    def second_matmul(inverse, done, emit):
        pairs = hid_tiles // 2
        for t in range(in_tiles):
            if t == in_tiles // 2:
                w2_copies[1].wait()
            for i in range(pairs):
                if t == 0 and i >= done:
                    finish(i, inverse)
                for unit in range(2):
                    k = 2 * i + unit
                    multiply(outs[t % 3][unit], hid[k], w2_v[tile_at(k), tile_at(t)], unit)
            if t > 0:
                emit(t - 1)
        emit(in_tiles - 1)

    def popped(t):
        return pltpu.matmul_pop(outs[t % 3][0]) + pltpu.matmul_pop(outs[t % 3][1])

    def place(base_ref, ids_ref, value_ref, picks, first, count):
        group = 16
        for m in range(micro):
            for g in range(tok_rows // group):
                ids = row_iota((group, 128)) + (m * total + g * group) + me * tok_rows
                masks = [(ids == ids_ref[r : r + 1, :], r) for r in picks(m)]
                at = slice(m * tok_rows + g * group, m * tok_rows + (g + 1) * group)
                for b in range(first * TILE // 128, (first + count) * TILE // 128):
                    span = slice(b * 128, (b + 1) * 128)
                    added = jnp.zeros((group, 128), F32)
                    for mask, r in masks:
                        added = jnp.where(mask, value_ref[r : r + 1, span], added)
                    out_v[at, span] = (base_ref[at, span].astype(F32) + added).astype(BF16)

    def whole_picks(m):
        return range(m * cap, (m + 1) * cap)

    def slot_picks(m):
        return range(m * slots, (m + 1) * slots)

    near = in_tiles // 2
    zero = jnp.zeros((items, 128), F32)

    @pl.when(section == 0)
    def _():
        pick_rows(0, near)
        pl.semaphore_wait(barrier, 2 * owners - 1)
        for c in row_sends(0, near):
            c.start()
        pick_rows(near, in_tiles - near)
        for c in row_sends(near, in_tiles - near):
            c.start()
        for c in small_copies[1:]:
            c.wait()
        all_of(rows_buf.at[pl.ds(0, owners - 1)], rows_ssem).wait()
        ids_copy = copy_to(ids_send, ids_recv, misc_ssem.at[0], misc_rsem.at[0], 1, me)
        ids_copy.start()
        all_of(w1_v, w1_sem).wait()
        w2_copies[0].wait()
        gathered_rows()
        early = row_iota((rows, 128)) < cap
        masks = [code_col == code for code in range(owners * slots)]
        stats = (zero, zero)
        xs = []
        for k in range(in_tiles):
            halves = []
            for b in range(TILE // 128):
                span = slice(k * TILE + b * 128, k * TILE + (b + 1) * 128)
                value = jnp.zeros((rows, 128), F32)
                for p in range(owners):
                    for s in range(slots):
                        q = p * each + s
                        both = xf_v[q : q + 1, span]
                        for m in range(1, micro):
                            after = xf_v[q + m * slots : q + m * slots + 1, span]
                            both = jnp.where(early, both, after)
                        value = jnp.where(masks[p * slots + s], both, value)
                halves.append(value)
            act = jnp.concatenate(halves, axis=1)
            act = jnp.concatenate([act, jnp.zeros((items - rows, TILE), F32)], axis=0)
            scaled, stats = scaled_tile(act, k, stats)
            xs.append(scaled)
        inverse, gate = closing(stats)
        pairs = hid_tiles // 2
        for i in range(pairs):
            for k in range(in_tiles):
                for unit in range(2):
                    n = 2 * i + unit
                    multiply(sums[n], xs[k], w1_v[tile_at(k), tile_at(n)], unit)
            if i > 0:
                finish(i - 1, inverse)

        def emit(t):
            part_send[:, tile_at(t)] = (popped(t)[:rows] * gate[:rows]).astype(BF16)
            for j, (first, count) in enumerate(send_pieces):
                if first + count - 1 == t:
                    span = tile_at(first, count)
                    for p in [peer(k) for k in range(owners - 1)] + [me]:
                        copy_to(
                            part_send.at[:, span], part_recv.at[me, :, span], part_ssem,
                            part_rsem.at[j], 1, p,
                        ).start()

        second_matmul(inverse, pairs - 1, emit)
        back = copy_to(c_v, c_recv, misc_ssem.at[1], misc_rsem.at[1], 0, me)
        back.wait_recv()
        place(tok_v, ids_send, c_recv, whole_picks, 0, in_tiles)
        all_of(part_recv, part_ssem).wait()
        ids_copy.wait_send()

    @pl.when(section != 0)
    def _():
        pick_rows(0, in_tiles)
        pl.semaphore_wait(barrier, 2 * owners - 1)
        copy_to(ids_send, ids_recv, misc_ssem.at[0], misc_rsem.at[0], 1, me).wait_recv()
        for c in row_sends(0, in_tiles):
            c.start()
        for c in small_copies[1:]:
            c.wait()
        all_of(rows_buf.at[pl.ds(0, owners - 1)], rows_ssem).wait()
        gathered_rows()
        early = lax.rem(row_iota((items, 128)), each) < slots
        match = [
            sum((item_id == ids_recv[m * cap + c : m * cap + c + 1, :]).astype(F32) for m in range(micro))
            for c in range(cap)
        ]
        all_of(w1_v, w1_sem).wait()
        w2_copies[0].wait()
        stats = (zero, zero)
        for j, (first, count) in enumerate(send_pieces):
            all_of(part_recv.at[:, :, tile_at(first, count)], part_rsem.at[j]).wait()
            for k in range(first, first + count):
                span = tile_at(k)
                contrib = part_recv[0, :, span].astype(F32)
                for p in range(1, owners):
                    contrib = contrib + part_recv[p, :, span].astype(F32)
                c_v[:, span] = contrib
                halves = []
                for b in range(TILE // 128):
                    inner = slice(k * TILE + b * 128, k * TILE + (b + 1) * 128)
                    act = xf_v[:, inner]
                    for c in range(cap):
                        both = c_v[c : c + 1, inner]
                        for m in range(1, micro):
                            both = jnp.where(early, both, c_v[m * cap + c : m * cap + c + 1, inner])
                        act = act + match[c] * both
                    halves.append(act.astype(BF16).astype(F32))
                scaled, stats = scaled_tile(jnp.concatenate(halves, axis=1), k, stats)
                for n in range(hid_tiles):
                    multiply(sums[n], scaled, w1_v[span, tile_at(n)], n % 2)
        back = copy_to(c_v, c_recv, misc_ssem.at[1], misc_rsem.at[1], 0, me)
        back.start()
        inverse, gate = closing(stats)

        def emit(t):
            value = popped(t) * gate
            for p in range(owners):
                last_send[p, :, tile_at(t)] = value[p * each : (p + 1) * each].astype(BF16)
            for j, (first, count) in enumerate(last_pieces):
                if first + count - 1 == t:
                    span = tile_at(first, count)
                    for p in [peer(k) for k in range(owners - 1)]:
                        copy_to(
                            last_send.at[p, :, span], last_recv.at[me, :, span], part_ssem,
                            last_rsem.at[j], 1, p,
                        ).start()

        second_matmul(inverse, 0, emit)
        place(tok_v, ids_recv, c_v, whole_picks, 0, in_tiles)
        for j, (first, count) in enumerate(last_pieces):
            span = tile_at(first, count)
            all_of(last_recv.at[pl.ds(0, owners - 1), :, span], last_rsem.at[j]).wait()
            value = last_send[me, :, span].astype(F32)
            for k in range(owners - 1):
                value = value + last_recv[peer(k), :, span].astype(F32)
            fin_v[:each, span] = value
            place(out_v, own_ref, fin_v, slot_picks, first, count)
        all_of(last_recv.at[pl.ds(0, owners - 1)], part_ssem).wait()
        back.wait_send()


def scoped_kernel(dims, *refs):
    hidden, width = dims[3], dims[2]
    items = dims[4] * dims[0] * dims[6]
    dma = pltpu.SemaphoreType.DMA
    shape = (items, TILE)
    pl.run_scoped(
        lambda sums, outs, *sems: relay_kernel(dims, *refs, sums, outs, *sems),
        tuple(pltpu.ACC(n % 2)(shape, F32) for n in range(max(hidden, width) // TILE)),
        tuple((pltpu.ACC(0)(shape, F32), pltpu.ACC(1)(shape, F32)) for _ in range(3)),
        dma((3,)),
        dma((dims[0],)),
        dma,
        dma((2,)),
        dma,
        dma,
        dma((2,)),
    )


def fused(tokens, chosen, norm_gain, router, w_in, w_out):
    micro, tok_rows, width = tokens.shape
    owners = lax.axis_size("expert")
    cap = chosen.shape[3]
    hidden = w_in.shape[3]
    rows = micro * cap
    slots = 2 * cap // owners
    each = micro * slots
    items = owners * each
    dims = (micro, tok_rows, width, hidden, owners, cap, slots)
    vmem = pl.BlockSpec(memory_space=pltpu.VMEM)
    hbm = pl.BlockSpec(memory_space=pltpu.HBM)
    dma = pltpu.SemaphoreType.DMA
    result = pl.pallas_call(
        functools.partial(scoped_kernel, dims),
        out_shape=pltpu.VMEM((micro * tok_rows, width), BF16),
        in_specs=[hbm] * 6,
        out_specs=vmem,
        scratch_shapes=[
            pltpu.SMEM((1, micro, 1, cap), jnp.int32),
            pltpu.VMEM((1, width), F32),
            pltpu.VMEM((1, width), BF16),
            pltpu.VMEM((TILE, width), BF16),
            pltpu.VMEM((width, hidden), BF16),
            pltpu.VMEM((hidden, width), BF16),
            pltpu.VMEM((owners, each, width), BF16),
            pltpu.VMEM((items, width), F32),
            pltpu.VMEM((rows, width), BF16),
            pltpu.VMEM((owners, rows, width), BF16),
            pltpu.VMEM((owners, each, width), BF16),
            pltpu.VMEM((owners, each, width), BF16),
            pltpu.VMEM((rows, width), F32),
            pltpu.VMEM((rows, width), F32),
            pltpu.VMEM((8, width), F32),
            pltpu.VMEM((rows, 128), jnp.int32),
            pltpu.VMEM((rows, 128), jnp.int32),
            pltpu.VMEM((items, 128), jnp.int32),
            dma,
            dma((len(pieces(SEND_TILES, width // TILE)),)),
            dma((len(pieces(LAST_TILES, width // TILE)),)),
            dma((2,)),
        ],
        compiler_params=pltpu.CompilerParams(
            collective_id=0, has_side_effects=True, vmem_limit_bytes=60 * 1024 * 1024
        ),
    )(tokens, chosen, norm_gain, router[:, :, 0], w_in, w_out)
    return result.reshape(1, micro, tok_rows, width)


def passed_along(value, axis, steps):
    count = lax.axis_size(axis)
    leading, last = (max(0, -steps), min(count, count - steps))
    return lax.ppermute(value, axis, [(source, source + steps) for source in range(leading, last)])


def moe_layer(
    current, picks_now, gain_row, router_cols, w_first, w_second, device, owners, shards_each
):
    tok_rows, width = current.shape
    experts, capacity = picks_now.shape
    slots = 2 * capacity // owners
    floats = current.astype(jnp.float32)
    inverse_rms = lax.rsqrt(jnp.mean(floats * floats, axis=-1, keepdims=True) + 1e-06)
    normed = (floats * inverse_rms * gain_row).astype(jnp.bfloat16)
    gate_all = jax.nn.sigmoid(jnp.dot(normed, router_cols, preferred_element_type=jnp.float32))
    owner_of = picks_now // tok_rows
    onehot = (owner_of[:, :, None] == jnp.arange(owners, dtype=jnp.int32)[None, None, :]).astype(
        jnp.int32
    )
    order_slot = jnp.cumsum(onehot, axis=1) - 1
    slot_of = jnp.sum(order_slot * onehot, axis=2)
    is_mine = owner_of == device
    local_idx = picks_now - device * tok_rows
    slot_hit = (
        (slot_of[:, :, None] == jnp.arange(slots, dtype=jnp.int32)[None, None, :])
        & is_mine[:, :, None]
    ).astype(jnp.float32)
    tok_hit = (
        local_idx[:, :, None] == jnp.arange(tok_rows, dtype=jnp.int32)[None, None, :]
    ).astype(jnp.float32)
    selector = jnp.einsum("xcs,xct->xst", slot_hit, tok_hit)
    flat_select = selector.reshape(experts * slots, tok_rows)
    gate_slot = jnp.einsum("xst,tx->xs", selector, gate_all, precision=lax.Precision.HIGHEST)
    dispatched = jnp.dot(
        flat_select.astype(jnp.bfloat16), normed, preferred_element_type=jnp.float32
    ).astype(jnp.bfloat16)
    outgoing = jnp.broadcast_to(
        dispatched.reshape(experts, 1, slots, width), (experts, shards_each, slots, width)
    ).reshape(owners, slots, width)
    arrived = lax.all_to_all(outgoing, "expert", split_axis=0, concat_axis=0, tiled=True)
    item_count = arrived.shape[1]
    flat_rows = arrived.reshape(-1, width)
    hidden = jax.nn.gelu(
        jnp.dot(flat_rows, w_first, preferred_element_type=jnp.float32), approximate=True
    ).astype(jnp.bfloat16)
    partial_value = jnp.dot(hidden, w_second, preferred_element_type=jnp.float32).reshape(
        owners, item_count, width
    )
    returned = lax.all_to_all(partial_value, "expert", split_axis=0, concat_axis=0, tiled=True)
    summed = returned.reshape(experts, shards_each, slots, width).sum(axis=1)
    weighted = summed * gate_slot[:, :, None]
    contrib = jnp.dot(
        flat_select.T, weighted.reshape(experts * slots, width), precision=lax.Precision.HIGHEST
    )
    return (floats + contrib).astype(jnp.bfloat16)


def fits(tokens, chosen, w_in, sections, owners):
    micro, tok_rows, width = tokens.shape
    experts, cap = chosen.shape[2:]
    hidden = w_in.shape[3]
    slots = 2 * cap // owners
    whole_tiles = width % 512 == 0 and hidden % 512 == 0 and hidden <= 2048 and width <= 2048
    few = micro == 2 and micro * cap == 8 and owners * micro * slots == 16
    return (
        sections == 2 and experts == 1 and whole_tiles and few
        and tok_rows % 16 == 0 and micro * tok_rows <= TILE
    )


def local(tokens, chosen, norm_gain, router, w_in, w_out):
    sections = lax.axis_size("section")
    owners = lax.axis_size("expert")
    if fits(tokens, chosen, w_in, sections, owners):
        return fused(tokens, chosen, norm_gain, router, w_in, w_out)
    section_index = lax.axis_index("section")
    device = lax.axis_index("expert")
    micro_count, tok_rows, width = tokens.shape
    experts = chosen.shape[2]
    shards_each = owners // experts
    gain_row = norm_gain[0]
    router_cols = router[0]
    w_first = w_in[0, 0]
    w_second = w_out[0, 0]
    outputs = jnp.zeros((1, micro_count, tok_rows, width), jnp.bfloat16)
    received = jnp.zeros((tok_rows, width), jnp.bfloat16)
    tick_count = micro_count + sections - 1
    for tick_index in range(tick_count):
        batch_index = tick_index - section_index
        clipped = jnp.clip(batch_index, 0, micro_count - 1)
        fresh_input = tokens[min(tick_index, micro_count - 1)]
        current = jnp.where(section_index == 0, fresh_input, received)
        picks_now = lax.dynamic_index_in_dim(chosen[0], clipped, 0, keepdims=False)
        layer_out = moe_layer(
            current,
            picks_now,
            gain_row,
            router_cols,
            w_first,
            w_second,
            device,
            owners,
            shards_each,
        )
        in_range = (batch_index >= 0) & (batch_index < micro_count)
        previous = lax.dynamic_index_in_dim(outputs[0], clipped, 0, keepdims=False)
        written = jnp.where(in_range, layer_out, previous)
        outputs = lax.dynamic_update_index_in_dim(outputs, written[None, None], clipped, 1)
        if tick_index + 1 < tick_count:
            received = passed_along(layer_out, "section", 1)
    return outputs


def solution(mesh):
    placed = (
        P("group", "expert", None),
        P("section", "group", None, None),
        P("section", None),
        P("section", None, None),
        P("section", "expert", None, None),
        P("section", "expert", None, None),
    )
    return jax.shard_map(
        local,
        mesh=mesh,
        in_specs=placed,
        out_specs=P("section", "group", "expert", None),
        check_vma=False,
    )
```

time: 20.1 us -> 18.7 us (0.930)
  Pallas kernels: 19.2 us -> 17.7 us
    pallas_call x1, Pallas kernels: 19.2 us -> 17.7 us  [fused(): pl.pallas_call(functools.partial(scoped_kernel, dims), out_shape=pltpu.VM...]
where the time goes in v2:
time: 18.7 us; the launch traced here: 18.5 us
  Pallas kernels  17.7 us (95%)
  local copies, waits for them, and re-layouts  0.8 us (4%)
    pallas_call x1, Pallas kernels, fused(): pl.pallas_call(functools.partial(scoped_kernel, dims), out_shape=pltpu.VM...  17.7 us
    unnamed x1, local copies, waits for them, and re-layouts  0.8 us

profile of v2, /device:TPU:1, one launch (start us, length us, event | category | flops | bytes accessed | tf_op | source)
XLA Modules:
  0.0 18.5 jit_solution(16201733264680597360)
XLA Ops:
  0.0 17.7 %shard_map.64 = bf16[128,2048]{1,0:T(8,128)(2,1)S(1)} custom-call(bf16[2,64,2048]{2,1,0:T(8,128)(2,1)} %refs_0_.1, s32[1,2,1,4]{3,2,1,0:T(1,128)} %refs_1_.1, f32[1,2048]{1,0:T(1,128)} %refs_2_.1, bf16[1,2048]{1,0:T(2,128)(2,1)} %bitcast.3, bf16[1,1,2048,2048]{3,2,1,0:T(8,128)(2,1)} %refs_4_.1, bf16[1,1,2048,2048]{3,2,1,0:T(8,128)(2,1)} %refs_5_.1), custom_call_target="tpu_custom_call" | custom-call | tf_op jit(solution)/shard_map/pallas_call | solution.py:465
  17.7 0.8 %copy.8 = bf16[1,2,64,2048]{3,2,1,0:T(8,128)(2,1)} copy(bf16[1,2,64,2048]{3,2,1,0:T(8,128)(2,1)S(1)} %bitcast.2) | data formatting | bytes 1048576

commit v3 on v2

--- a/solution.py
+++ b/solution.py
@@ -11,7 +11,7 @@
 BF16 = jnp.bfloat16
 EPS = 1e-06
 TILE = 256
-SEND_TILES = (1, 1, 2, 2, 1, 1)
+SEND_TILES = (1, 1, 1, 1, 1, 1, 1, 1)
 LAST_TILES = (2, 2, 2, 1, 1)
 
 
@@ -53,6 +53,8 @@
     gain_ref,
     router_ref,
     tok_v,
+    tf_v,
+    pick_v,
     w1_v,
     w2_v,
     rows_buf,
@@ -67,12 +69,12 @@
     ids_send,
     ids_recv,
     own_ref,
+    sums,
+    outs,
     rows_rsem,
     part_rsem,
     last_rsem,
     misc_rsem,
-    sums,
-    outs,
     small_sem,
     tok_sem,
     w1_sem,
@@ -114,11 +116,18 @@
 
     staged = [0, 0]
 
-    def multiply(acc, lhs, rhs, unit):
+    waiting = ([], [])
+
+    def push(rhs, unit):
         register = staged[unit]
         staged[unit] = 1 - register
         pltpu.matmul_push_rhs(rhs, staging_register=register, mxu_index=unit)
-        pltpu.matmul_acc_lhs(acc, lhs, load_staged_rhs=register)
+        waiting[unit].append(register)
+
+    def multiply(acc, lhs, rhs, unit):
+        if rhs is not None:
+            push(rhs, unit)
+        pltpu.matmul_acc_lhs(acc, lhs, load_staged_rhs=waiting[unit].pop(0))
 
     barrier = pltpu.get_barrier_semaphore()
     for o in range(1, owners):
@@ -164,14 +173,15 @@
         )
         for k in range(2)
     ]
-    if tokens < TILE:
-        tok_v[tokens:, :] = jnp.zeros((TILE - tokens, width), BF16)
 
     small_copies[0].wait()
+    for c in w1_copies + w2_copies:
+        c.start()
     id_col = jnp.full((rows, 128), -1, jnp.int32)
     code_col = jnp.full((rows, 128), -1, jnp.int32)
     item_id = jnp.full((items, 128), -1, jnp.int32)
     own_id = jnp.full((items, 128), -1, jnp.int32)
+    spots = [jnp.int32(0)] * each
     for m in range(micro):
         owner_of = []
         for c in range(cap):
@@ -188,39 +198,30 @@
             code_col = jnp.where(row_iota((rows, 128)) == r, owner * slots + slot, code_col)
             item_id = jnp.where(row_iota((items, 128)) == owner * each + inner, ident, item_id)
             at = jnp.where(owner == me, inner, -1)
+            local = pick + (m - owner) * tok_rows
+            for k in range(each):
+                spots[k] = jnp.where(at == k, local, spots[k])
             own_id = jnp.where(row_iota((items, 128)) == at, ident, own_id)
     ids_send[...] = id_col
     own_ref[...] = own_id
 
-    lanes = lane_iota((items, TILE))
-    lane_id = lanes + me * tok_rows
-    for m in range(1, micro):
-        lane_id = lane_id + jnp.where(lanes >= m * tok_rows, total - tok_rows, 0)
-    lane_id = jnp.where(lanes < tokens, lane_id, -2)
-    pick_lhs = (
-        (lane_id == jnp.concatenate([own_id] * (TILE // 128), axis=1)).astype(F32).astype(BF16)
-    )
-
     for c in tok_copies:
         c.wait()
-    for c in w1_copies + w2_copies:
-        c.start()
 
     def pick_rows(first, count):
-        for n in range(first, first + count):
-            multiply(sums[n], pick_lhs, tok_v[:, tile_at(n)], n % 2)
-        for n in range(first, first + count):
-            rows_buf[me, :, tile_at(n)] = pltpu.matmul_pop(sums[n])[:each].astype(BF16)
-
-    def row_sends(first, count):
         span = tile_at(first, count)
-        return [
-            copy_to(
-                rows_buf.at[me, :, span], rows_buf.at[me, :, span], rows_ssem, rows_rsem,
-                section, peer(k),
-            )
-            for k in range(owners - 1)
-        ]
+        tf_v[:, span] = tok_v[:, span].astype(F32)
+        for m in range(micro):
+            for k in range(slots):
+                found = tf_v[pl.ds(spots[m * slots + k], 1), span]
+                pick_v[m * slots + k : m * slots + k + 1, span] = found
+        rows_buf[me, :, span] = pick_v[:each, span].astype(BF16)
+
+    def row_send(to, first, count):
+        span = tile_at(first, count)
+        copy_to(
+            rows_buf.at[me, :, span], rows_buf.at[me, :, span], rows_ssem, rows_rsem, section, to
+        ).start()
 
     def gathered_rows():
         all_of(rows_buf.at[pl.ds(0, owners - 1)], rows_rsem).wait()
@@ -296,11 +297,11 @@
     def _():
         pick_rows(0, near)
         pl.semaphore_wait(barrier, 2 * owners - 1)
-        for c in row_sends(0, near):
-            c.start()
+        row_send(peer(0), 0, near)
         pick_rows(near, in_tiles - near)
-        for c in row_sends(near, in_tiles - near):
-            c.start()
+        row_send(peer(0), near, in_tiles - near)
+        for k in range(1, owners - 1):
+            row_send(peer(k), 0, in_tiles)
         for c in small_copies[1:]:
             c.wait()
         all_of(rows_buf.at[pl.ds(0, owners - 1)], rows_ssem).wait()
@@ -308,6 +309,9 @@
         ids_copy.start()
         all_of(w1_v, w1_sem).wait()
         w2_copies[0].wait()
+        for k in range(2):
+            for unit in range(2):
+                push(w1_v[tile_at(k), tile_at(unit)], unit)
         gathered_rows()
         early = row_iota((rows, 128)) < cap
         masks = [code_col == code for code in range(owners * slots)]
@@ -337,7 +341,9 @@
             for k in range(in_tiles):
                 for unit in range(2):
                     n = 2 * i + unit
-                    multiply(sums[n], xs[k], w1_v[tile_at(k), tile_at(n)], unit)
+                    ready = i == 0 and k < 2
+                    rhs = None if ready else w1_v[tile_at(k), tile_at(n)]
+                    multiply(sums[n], xs[k], rhs, unit)
             if i > 0:
                 finish(i - 1, inverse)
 
@@ -364,8 +370,8 @@
         pick_rows(0, in_tiles)
         pl.semaphore_wait(barrier, 2 * owners - 1)
         copy_to(ids_send, ids_recv, misc_ssem.at[0], misc_rsem.at[0], 1, me).wait_recv()
-        for c in row_sends(0, in_tiles):
-            c.start()
+        for k in range(owners - 1):
+            row_send(peer(k), 0, in_tiles)
         for c in small_copies[1:]:
             c.wait()
         all_of(rows_buf.at[pl.ds(0, owners - 1)], rows_ssem).wait()
@@ -377,6 +383,8 @@
         ]
         all_of(w1_v, w1_sem).wait()
         w2_copies[0].wait()
+        for n in range(4):
+            push(w1_v[tile_at(0), tile_at(n)], n % 2)
         stats = (zero, zero)
         for j, (first, count) in enumerate(send_pieces):
             all_of(part_recv.at[:, :, tile_at(first, count)], part_rsem.at[j]).wait()
@@ -398,7 +406,10 @@
                     halves.append(act.astype(BF16).astype(F32))
                 scaled, stats = scaled_tile(jnp.concatenate(halves, axis=1), k, stats)
                 for n in range(hid_tiles):
-                    multiply(sums[n], scaled, w1_v[span, tile_at(n)], n % 2)
+                    multiply(sums[n], scaled, None if n < 4 else w1_v[span, tile_at(n)], n % 2)
+                if k + 1 < in_tiles:
+                    for n in range(4):
+                        push(w1_v[tile_at(k + 1), tile_at(n)], n % 2)
         back = copy_to(c_v, c_recv, misc_ssem.at[1], misc_rsem.at[1], 0, me)
         back.start()
         inverse, gate = closing(stats)
@@ -439,6 +450,10 @@
         lambda sums, outs, *sems: relay_kernel(dims, *refs, sums, outs, *sems),
         tuple(pltpu.ACC(n % 2)(shape, F32) for n in range(max(hidden, width) // TILE)),
         tuple((pltpu.ACC(0)(shape, F32), pltpu.ACC(1)(shape, F32)) for _ in range(3)),
+        dma,
+        dma((len(pieces(SEND_TILES, width // TILE)),)),
+        dma((len(pieces(LAST_TILES, width // TILE)),)),
+        dma((2,)),
         dma((3,)),
         dma((dims[0],)),
         dma,
@@ -461,7 +476,6 @@
     dims = (micro, tok_rows, width, hidden, owners, cap, slots)
     vmem = pl.BlockSpec(memory_space=pltpu.VMEM)
     hbm = pl.BlockSpec(memory_space=pltpu.HBM)
-    dma = pltpu.SemaphoreType.DMA
     result = pl.pallas_call(
         functools.partial(scoped_kernel, dims),
         out_shape=pltpu.VMEM((micro * tok_rows, width), BF16),
@@ -471,7 +485,9 @@
             pltpu.SMEM((1, micro, 1, cap), jnp.int32),
             pltpu.VMEM((1, width), F32),
             pltpu.VMEM((1, width), BF16),
-            pltpu.VMEM((TILE, width), BF16),
+            pltpu.VMEM((micro * tok_rows, width), BF16),
+            pltpu.VMEM((micro * tok_rows, width), F32),
+            pltpu.VMEM((8, width), F32),
             pltpu.VMEM((width, hidden), BF16),
             pltpu.VMEM((hidden, width), BF16),
             pltpu.VMEM((owners, each, width), BF16),
@@ -486,10 +502,6 @@
             pltpu.VMEM((rows, 128), jnp.int32),
             pltpu.VMEM((rows, 128), jnp.int32),
             pltpu.VMEM((items, 128), jnp.int32),
-            dma,
-            dma((len(pieces(SEND_TILES, width // TILE)),)),
-            dma((len(pieces(LAST_TILES, width // TILE)),)),
-            dma((2,)),
         ],
         compiler_params=pltpu.CompilerParams(
             collective_id=0, has_side_effects=True, vmem_limit_bytes=60 * 1024 * 1024

time: 18.7 us -> 18.2 us (0.973)
  Pallas kernels: 17.7 us -> 17.2 us
    pallas_call x1, Pallas kernels: 17.7 us -> 17.2 us  [fused(): pl.pallas_call(functools.partial(scoped_kernel, dims), out_shape=pltpu.VM...]
where the time goes in v3:
time: 18.2 us; the launch traced here: 18 us
  Pallas kernels  17.2 us (95%)
  local copies, waits for them, and re-layouts  0.8 us (4%)
    pallas_call x1, Pallas kernels, fused(): pl.pallas_call(functools.partial(scoped_kernel, dims), out_shape=pltpu.VM...  17.2 us
    unnamed x1, local copies, waits for them, and re-layouts  0.8 us

profile of v3, /device:TPU:1, one launch (start us, length us, event | category | flops | bytes accessed | tf_op | source)
XLA Modules:
  0.0 18.0 jit_solution(1156814954046311253)
XLA Ops:
  0.0 17.2 %shard_map.64 = bf16[128,2048]{1,0:T(8,128)(2,1)S(1)} custom-call(bf16[2,64,2048]{2,1,0:T(8,128)(2,1)} %refs_0_.1, s32[1,2,1,4]{3,2,1,0:T(1,128)} %refs_1_.1, f32[1,2048]{1,0:T(1,128)} %refs_2_.1, bf16[1,2048]{1,0:T(2,128)(2,1)} %bitcast.3, bf16[1,1,2048,2048]{3,2,1,0:T(8,128)(2,1)} %refs_4_.1, bf16[1,1,2048,2048]{3,2,1,0:T(8,128)(2,1)} %refs_5_.1), custom_call_target="tpu_custom_call" | custom-call | tf_op jit(solution)/shard_map/pallas_call | solution.py:479
  17.3 0.8 %copy.8 = bf16[1,2,64,2048]{3,2,1,0:T(8,128)(2,1)} copy(bf16[1,2,64,2048]{3,2,1,0:T(8,128)(2,1)S(1)} %bitcast.2) | data formatting | bytes 1048576

commit v4 on v3

--- a/solution.py
+++ b/solution.py
@@ -11,8 +11,8 @@
 BF16 = jnp.bfloat16
 EPS = 1e-06
 TILE = 256
-SEND_TILES = (1, 1, 1, 1, 1, 1, 1, 1)
-LAST_TILES = (2, 2, 2, 1, 1)
+LAG = 2
+LAST_TILES = (3, 3, 1, 1)
 
 
 def row_iota(shape):
@@ -90,7 +90,7 @@
     total = owners * tok_rows
     tokens = micro * tok_rows
     in_tiles, hid_tiles = width // TILE, hidden // TILE
-    send_pieces = pieces(SEND_TILES, in_tiles)
+    send_pieces = pieces((), in_tiles)
     last_pieces = pieces(LAST_TILES, in_tiles)
     section = lax.axis_index("section")
     me = lax.axis_index("expert")
@@ -146,9 +146,10 @@
         )
     tok_copies = [
         pltpu.make_async_copy(
-            tok_hbm.at[m], tok_v.at[pl.ds(m * tok_rows, tok_rows)], tok_sem.at[m]
+            tok_hbm.at[m, pl.ds(g, 8)], tok_v.at[pl.ds(m * tok_rows + g, 8)], tok_sem.at[0]
         )
         for m in range(micro)
+        for g in range(0, tok_rows, 8)
     ]
     small_copies = [
         pltpu.make_async_copy(chosen_hbm, chosen_ref, small_sem.at[0]),
@@ -205,8 +206,7 @@
     ids_send[...] = id_col
     own_ref[...] = own_id
 
-    for c in tok_copies:
-        c.wait()
+    all_of(tok_v.at[pl.ds(0, tokens)], tok_sem.at[0]).wait()
 
     def pick_rows(first, count):
         span = tile_at(first, count)
@@ -347,16 +347,20 @@
             if i > 0:
                 finish(i - 1, inverse)
 
+        def part_start(t, to):
+            span = tile_at(t)
+            copy_to(
+                part_send.at[:, span], part_recv.at[me, :, span], part_ssem, part_rsem.at[t], 1, to
+            ).start()
+
         def emit(t):
             part_send[:, tile_at(t)] = (popped(t)[:rows] * gate[:rows]).astype(BF16)
-            for j, (first, count) in enumerate(send_pieces):
-                if first + count - 1 == t:
-                    span = tile_at(first, count)
-                    for p in [peer(k) for k in range(owners - 1)] + [me]:
-                        copy_to(
-                            part_send.at[:, span], part_recv.at[me, :, span], part_ssem,
-                            part_rsem.at[j], 1, p,
-                        ).start()
+            part_start(t, peer(0))
+            part_start(t, me)
+            for late in range(in_tiles):
+                if min(late + LAG, in_tiles - 1) == t:
+                    for k in range(1, owners - 1):
+                        part_start(late, peer(k))
 
         second_matmul(inverse, pairs - 1, emit)
         back = copy_to(c_v, c_recv, misc_ssem.at[1], misc_rsem.at[1], 0, me)
@@ -383,7 +387,7 @@
         ]
         all_of(w1_v, w1_sem).wait()
         w2_copies[0].wait()
-        for n in range(4):
+        for n in range(2):
             push(w1_v[tile_at(0), tile_at(n)], n % 2)
         stats = (zero, zero)
         for j, (first, count) in enumerate(send_pieces):
@@ -406,9 +410,9 @@
                     halves.append(act.astype(BF16).astype(F32))
                 scaled, stats = scaled_tile(jnp.concatenate(halves, axis=1), k, stats)
                 for n in range(hid_tiles):
-                    multiply(sums[n], scaled, None if n < 4 else w1_v[span, tile_at(n)], n % 2)
+                    multiply(sums[n], scaled, None if n < 2 else w1_v[span, tile_at(n)], n % 2)
                 if k + 1 < in_tiles:
-                    for n in range(4):
+                    for n in range(2):
                         push(w1_v[tile_at(k + 1), tile_at(n)], n % 2)
         back = copy_to(c_v, c_recv, misc_ssem.at[1], misc_rsem.at[1], 0, me)
         back.start()
@@ -451,7 +455,7 @@
         tuple(pltpu.ACC(n % 2)(shape, F32) for n in range(max(hidden, width) // TILE)),
         tuple((pltpu.ACC(0)(shape, F32), pltpu.ACC(1)(shape, F32)) for _ in range(3)),
         dma,
-        dma((len(pieces(SEND_TILES, width // TILE)),)),
+        dma((width // TILE,)),
         dma((len(pieces(LAST_TILES, width // TILE)),)),
         dma((2,)),
         dma((3,)),

time: 18.2 us -> 18.1 us (level)
  no operation moved by 1% of the time
where the time goes in v4:
time: 18.1 us; the launch traced here: 18 us
  Pallas kernels  17.2 us (95%)
  local copies, waits for them, and re-layouts  0.8 us (4%)
    pallas_call x1, Pallas kernels, fused(): pl.pallas_call(functools.partial(scoped_kernel, dims), out_shape=pltpu.VM...  17.2 us
    unnamed x1, local copies, waits for them, and re-layouts  0.8 us

profile of v4, /device:TPU:1, one launch (start us, length us, event | category | flops | bytes accessed | tf_op | source)
XLA Modules:
  0.0 18.0 jit_solution(14233679476676959668)
XLA Ops:
  0.0 17.2 %shard_map.64 = bf16[128,2048]{1,0:T(8,128)(2,1)S(1)} custom-call(bf16[2,64,2048]{2,1,0:T(8,128)(2,1)} %refs_0_.1, s32[1,2,1,4]{3,2,1,0:T(1,128)} %refs_1_.1, f32[1,2048]{1,0:T(1,128)} %refs_2_.1, bf16[1,2048]{1,0:T(2,128)(2,1)} %bitcast.3, bf16[1,1,2048,2048]{3,2,1,0:T(8,128)(2,1)} %refs_4_.1, bf16[1,1,2048,2048]{3,2,1,0:T(8,128)(2,1)} %refs_5_.1), custom_call_target="tpu_custom_call" | custom-call | tf_op jit(solution)/shard_map/pallas_call | solution.py:483
  17.2 0.8 %copy.8 = bf16[1,2,64,2048]{3,2,1,0:T(8,128)(2,1)} copy(bf16[1,2,64,2048]{3,2,1,0:T(8,128)(2,1)S(1)} %bitcast.2) | data formatting | bytes 1048576

commit v5 on v4

--- a/solution.py
+++ b/solution.py
@@ -220,11 +220,12 @@
     def row_send(to, first, count):
         span = tile_at(first, count)
         copy_to(
-            rows_buf.at[me, :, span], rows_buf.at[me, :, span], rows_ssem, rows_rsem, section, to
+            rows_buf.at[me, :, span], rows_buf.at[me, :, span], rows_ssem, rows_rsem.at[me], section, to
         ).start()
 
     def gathered_rows():
-        all_of(rows_buf.at[pl.ds(0, owners - 1)], rows_rsem).wait()
+        for k in range(owners - 1):
+            all_of(rows_buf.at[peer(k)], rows_rsem.at[peer(k)]).wait()
         for p in range(owners):
             xf_v[p * each : (p + 1) * each, :] = rows_buf[p].astype(F32)
 
@@ -290,16 +291,13 @@
     def slot_picks(m):
         return range(m * slots, (m + 1) * slots)
 
-    near = in_tiles // 2
     zero = jnp.zeros((items, 128), F32)
 
     @pl.when(section == 0)
     def _():
-        pick_rows(0, near)
+        pick_rows(0, in_tiles)
         pl.semaphore_wait(barrier, 2 * owners - 1)
-        row_send(peer(0), 0, near)
-        pick_rows(near, in_tiles - near)
-        row_send(peer(0), near, in_tiles - near)
+        row_send(peer(0), 0, in_tiles)
         for k in range(1, owners - 1):
             row_send(peer(k), 0, in_tiles)
         for c in small_copies[1:]:
@@ -312,26 +310,38 @@
         for k in range(2):
             for unit in range(2):
                 push(w1_v[tile_at(k), tile_at(unit)], unit)
-        gathered_rows()
         early = row_iota((rows, 128)) < cap
-        masks = [code_col == code for code in range(owners * slots)]
+
+        def chosen_rows(value, j, owner, span):
+            for s in range(slots):
+                q = j * each + s
+                both = xf_v[q : q + 1, span]
+                for m in range(1, micro):
+                    after = xf_v[q + m * slots : q + m * slots + 1, span]
+                    both = jnp.where(early, both, after)
+                value = jnp.where(code_col == owner * slots + s, both, value)
+            return value
+
+        spans = [slice(b * 128, (b + 1) * 128) for b in range(width // 128)]
+        order = [me] + [peer(owners - 2 - k) for k in range(owners - 1)]
+        for j, owner in enumerate(order):
+            if j > 0:
+                all_of(rows_buf.at[owner], rows_rsem.at[owner]).wait()
+            xf_v[j * each : (j + 1) * each, :] = rows_buf[owner].astype(F32)
+            if j + 1 < owners:
+                for span in spans:
+                    start = c_v[:, span] if j > 0 else jnp.zeros((rows, 128), F32)
+                    c_v[:, span] = chosen_rows(start, j, owner, span)
         stats = (zero, zero)
         xs = []
         for k in range(in_tiles):
-            halves = []
-            for b in range(TILE // 128):
-                span = slice(k * TILE + b * 128, k * TILE + (b + 1) * 128)
-                value = jnp.zeros((rows, 128), F32)
-                for p in range(owners):
-                    for s in range(slots):
-                        q = p * each + s
-                        both = xf_v[q : q + 1, span]
-                        for m in range(1, micro):
-                            after = xf_v[q + m * slots : q + m * slots + 1, span]
-                            both = jnp.where(early, both, after)
-                        value = jnp.where(masks[p * slots + s], both, value)
-                halves.append(value)
-            act = jnp.concatenate(halves, axis=1)
+            act = jnp.concatenate(
+                [
+                    chosen_rows(c_v[:, span], owners - 1, order[-1], span)
+                    for span in spans[k * TILE // 128 : (k + 1) * TILE // 128]
+                ],
+                axis=1,
+            )
             act = jnp.concatenate([act, jnp.zeros((items - rows, TILE), F32)], axis=0)
             scaled, stats = scaled_tile(act, k, stats)
             xs.append(scaled)
@@ -454,7 +464,7 @@
         lambda sums, outs, *sems: relay_kernel(dims, *refs, sums, outs, *sems),
         tuple(pltpu.ACC(n % 2)(shape, F32) for n in range(max(hidden, width) // TILE)),
         tuple((pltpu.ACC(0)(shape, F32), pltpu.ACC(1)(shape, F32)) for _ in range(3)),
-        dma,
+        dma((dims[4],)),
         dma((width // TILE,)),
         dma((len(pieces(LAST_TILES, width // TILE)),)),
         dma((2,)),

time: 18.1 us -> 18.2 us (level)
  no operation moved by 1% of the time
where the time goes in v5:
time: 18.2 us; the launch traced here: 18 us
  Pallas kernels  17.2 us (95%)
  local copies, waits for them, and re-layouts  0.8 us (4%)
    pallas_call x1, Pallas kernels, fused(): pl.pallas_call(functools.partial(scoped_kernel, dims), out_shape=pltpu.VM...  17.2 us
    unnamed x1, local copies, waits for them, and re-layouts  0.8 us

profile of v5, /device:TPU:1, one launch (start us, length us, event | category | flops | bytes accessed | tf_op | source)
XLA Modules:
  0.0 18.0 jit_solution(4037489833541957284)
XLA Ops:
  0.0 17.2 %shard_map.64 = bf16[128,2048]{1,0:T(8,128)(2,1)S(1)} custom-call(bf16[2,64,2048]{2,1,0:T(8,128)(2,1)} %refs_0_.1, s32[1,2,1,4]{3,2,1,0:T(1,128)} %refs_1_.1, f32[1,2048]{1,0:T(1,128)} %refs_2_.1, bf16[1,2048]{1,0:T(2,128)(2,1)} %bitcast.3, bf16[1,1,2048,2048]{3,2,1,0:T(8,128)(2,1)} %refs_4_.1, bf16[1,1,2048,2048]{3,2,1,0:T(8,128)(2,1)} %refs_5_.1), custom_call_target="tpu_custom_call" | custom-call | tf_op jit(solution)/shard_map/pallas_call | solution.py:493
  17.2 0.8 %copy.8 = bf16[1,2,64,2048]{3,2,1,0:T(8,128)(2,1)} copy(bf16[1,2,64,2048]{3,2,1,0:T(8,128)(2,1)S(1)} %bitcast.2) | data formatting | bytes 1048576
